TPU v7x, 32 devices: a whole 2x2x4 slice. The times are simulated.
32 devices in a mesh: grp: 2 (over y), gz: 4 (over z), gx: 2 (over x), row: 2 (over core).
Axes of the slice: x: 2, y: 2, z: 4, core: 2. Of those that a mesh axis runs over, the one named last changes fastest.
Arguments:
- volume: float32 [32, 512, 512], P(('grp', 'gz'), 'gx', 'row'), parts along dimension 0, may hold values from -6 to 6
- tile_table: bfloat16 [64, 128, 128], replicated, may hold values from -0.09375 to 0.09375
- tile_ids: int32 [4, 2, 2, 4, 32], P('gz', 'gx', 'row'), may hold values from 0 to 63
- block_ids: int32 [4, 2, 2, 4, 768], P('gz', 'gx', 'row'), may hold values from 0 to 2047
- live_slots: int32 [4, 2, 2, 4], P('gz', 'gx', 'row'), may hold values from 4 to 32, as said below
- measured: float32 [8, 512, 16], P(('grp', 'gz'), ('gx', 'row')), parts along dimension 0, may hold values from -12 to 12
- row_norm: float32 [4, 512, 16], P('gz', ('gx', 'row')), may hold values from 0.2 to 1
- col_norm: float32 [16, 512, 512], P('gz', 'gx', 'row'), may hold values from 0.5 to 2
Outputs:
- new_volume: float32 [32, 512, 512], P(('grp', 'gz'), 'gx', 'row'), parts along dimension 0
There are 2 independent parts, one for each index of `grp`. A program takes and returns all parts, laid end to end along the dimension named above; an argument that names none is the same for every part. Nothing has to cross between parts.
Inputs may be any that keep to these rules, and one draw needn't show every extreme that they name: `block_ids`: indices of voxel blocks of the piece itself. `live_slots`: 32 is reached by some angle of some piece in every draw.
All inputs are finite; a program needn't handle non-finite values.
Results may differ from a plain program's by a relative error of at most 0.004.
Values may be sent and summed in bfloat16 or wider, within the bound.
A program may use at most 64 MiB of HBM per device.

v0:
```python
import math
import jax
import jax.numpy as jnp
from jax import lax
from jax.sharding import PartitionSpec as P


def extended_2(cells, sides, width):
    for axis, dim in sides:
        count = lax.axis_size(axis)
        ends = count - 1
        head = lax.slice_in_dim(cells, 0, width, axis=dim)
        tail = lax.slice_in_dim(cells, cells.shape[dim] - width, cells.shape[dim], axis=dim)
        cells = jnp.concatenate(
            [
                lax.ppermute(tail, axis, [(i, (i + 1) % count) for i in range(ends)]),
                cells,
                lax.ppermute(head, axis, [((i + 1) % count, i) for i in range(ends)]),
            ],
            axis=dim,
        )
    return cells


def slot_loop(slot_step, initial, tile_rows, block_rows, live_rows):
    slot_count = tile_rows.shape[1]
    position = jnp.arange(slot_count, dtype=jnp.int32)
    in_use = position[None, :] < live_rows[:, None]
    return slot_step(initial, tile_rows, block_rows, in_use)


def to_windows(row_data, slab_count, slab_depth):
    angles, columns, total_rows = row_data.shape
    padded = jnp.pad(row_data, ((0, 0), (0, 0), (1, 1)))
    head_rows = padded[:, :, :total_rows].reshape(angles, columns, slab_count, slab_depth)
    tail_rows = padded[:, :, 2:].reshape(angles, columns, slab_count, slab_depth)[
        :, :, :, slab_depth - 2 :
    ]
    joined = jnp.concatenate([head_rows, tail_rows], axis=3)
    return joined.transpose(0, 2, 1, 3)


def on_device(volume, tile_table, tile_ids, block_ids, live_slots, measured, row_norm, col_norm):
    slab_depth, column_width, half_width = volume.shape
    tile_count, tile_size = (tile_table.shape[0], tile_table.shape[1])
    angle_count = tile_ids.shape[3]
    slot_count = tile_ids.shape[4]
    window = slab_depth + 2
    block_cols = block_ids.shape[4] // (slot_count * window)
    det_width = block_cols * tile_size
    block_count = slab_depth * column_width * half_width // tile_size
    voxel_rows = volume.astype(jnp.bfloat16).reshape(block_count, tile_size)
    angle_block = math.gcd(angle_count, 2)
    step_count = angle_count // angle_block
    tile_steps = tile_ids.reshape(step_count, angle_block, slot_count)
    block_steps = block_ids.reshape(step_count, angle_block, slot_count, window, block_cols)
    live_steps = live_slots.reshape(step_count, angle_block)
    tile_numbers = jnp.arange(tile_count, dtype=jnp.int32)
    block_numbers = jnp.arange(block_count, dtype=jnp.int32)

    def pick_tiles(tile_part):
        tile_hot = (tile_part[:, :, None] == tile_numbers[None, None, :]).astype(jnp.bfloat16)
        picked = jnp.einsum(
            "akt,tdv->akdv", tile_hot, tile_table, preferred_element_type=jnp.float32
        )
        return picked.astype(jnp.bfloat16)

    def block_table(block_part, in_use):
        matches = block_part[:, :, :, :, None] == block_numbers[None, None, None, None, :]
        return (matches & in_use[:, :, None, None, None]).astype(jnp.bfloat16)

    slab_count = lax.axis_size("gz")
    own_angles, local_cols = (measured.shape[0], measured.shape[1])
    measured_win = to_windows(measured, slab_count, slab_depth).reshape(
        own_angles, slab_count, local_cols * window
    )
    norm_win = to_windows(row_norm, slab_count, slab_depth).reshape(
        own_angles, slab_count, local_cols * window
    )
    arrived = (
        lax.all_to_all(measured_win, "gz", split_axis=1, concat_axis=0, tiled=True),
        lax.all_to_all(norm_win, "gz", split_axis=1, concat_axis=0, tiled=True),
    )
    spread_out = (
        lax.all_gather(
            arrived[0].reshape(angle_count, local_cols * window), ("gx", "row"), axis=1, tiled=True
        ),
        lax.all_gather(
            arrived[1].reshape(angle_count, local_cols * window), ("gx", "row"), axis=1, tiled=True
        ),
    )
    target = spread_out[0].reshape(angle_count, det_width, window).transpose(0, 2, 1)
    weights = spread_out[1].reshape(angle_count, det_width, window).transpose(0, 2, 1)
    out_shape = (window, block_cols, tile_size)

    def project_angle_step(unused, inputs):
        tile_rows, block_rows, live_rows = inputs

        def slot_step(running, tile_part, block_part, in_use):
            picked = pick_tiles(tile_part)
            block_hot = block_table(block_part, in_use)
            voxels = jnp.einsum(
                "akwqn,nv->akwqv", block_hot, voxel_rows, preferred_element_type=jnp.float32
            )
            voxels = voxels.astype(jnp.bfloat16)
            return jnp.einsum(
                "akdv,akwqv->awqd", picked, voxels, preferred_element_type=jnp.float32
            )

        initial = jnp.zeros((angle_block,) + out_shape, jnp.float32)
        return (unused, slot_loop(slot_step, initial, tile_rows, block_rows, live_rows))

    ignored, stacked = lax.scan(
        project_angle_step, jnp.int32(0), (tile_steps, block_steps, live_steps)
    )
    partial_value = stacked.reshape((angle_count,) + out_shape).reshape(
        angle_count, window, det_width
    )
    total_proj = lax.psum(partial_value, ("gx", "row"))
    extended = extended_2(total_proj, (("gz", 1),), 2)
    folded = (
        total_proj.at[:, :2].add(extended[:, :2]).at[:, window - 2 :].add(extended[:, window + 2 :])
    )
    residual = (weights * (target - folded)).astype(jnp.bfloat16)
    res_steps = residual.reshape(step_count, angle_block, window, block_cols, tile_size)

    def back_angle_step(running_sum, inputs):
        tile_rows, block_rows, live_rows, res_rows = inputs

        def slot_step(running, tile_part, block_part, in_use):
            picked = pick_tiles(tile_part)
            block_hot = block_table(block_part, in_use)
            spread = jnp.einsum(
                "akdv,awqd->akwqv", picked, res_rows, preferred_element_type=jnp.float32
            )
            upper_part = spread.astype(jnp.bfloat16)
            lower_part = (spread - upper_part.astype(jnp.float32)).astype(jnp.bfloat16)
            added = jnp.einsum(
                "akwqn,akwqv->nv", block_hot, upper_part, preferred_element_type=jnp.float32
            )
            added = added + jnp.einsum(
                "akwqn,akwqv->nv", block_hot, lower_part, preferred_element_type=jnp.float32
            )
            return running + added

        return (slot_loop(slot_step, running_sum, tile_rows, block_rows, live_rows), None)

    initial = jnp.zeros((block_count, tile_size), jnp.float32)
    result, ignored = lax.scan(
        back_angle_step, initial, (tile_steps, block_steps, live_steps, res_steps)
    )
    return volume + col_norm * result.reshape(slab_depth, column_width, half_width)


def solution(mesh):
    placed = (
        P(("grp", "gz"), "gx", "row"),
        P(),
        P("gz", "gx", "row", None, None),
        P("gz", "gx", "row", None, None),
        P("gz", "gx", "row", None),
        P(("grp", "gz"), ("gx", "row"), None),
        P("gz", ("gx", "row"), None),
        P("gz", "gx", "row"),
    )
    return jax.shard_map(
        on_device,
        mesh=mesh,
        in_specs=placed,
        out_specs=P(("grp", "gz"), "gx", "row"),
        check_vma=False,
    )
```

profile of v0, /device:TPU:0, one launch (start us, length us, event | category | flops | bytes accessed | tf_op | source)
XLA Modules:
  0.0 91.1 jit_solution(14383756225101299012)
XLA Ops:
  0.0 3.0 %copy.90 = bf16[64,128,128]{2,0,1:T(8,128)(2,1)S(1)} copy(bf16[64,128,128]{2,1,0:T(8,128)(2,1)} %param.17) | data formatting | bytes 4194304
  3.0 0.2 reshape.178
  3.2 0.2 copy.89
  3.4 0.5 broadcast.83
  3.9 0.7 reduce.9
  4.6 0.1 reshape.179
  4.7 1.3 %convert_element_type.31 = bf16[4,256,256]{2,1,0:T(8,128)(2,1)S(1)} convert(f32[4,256,256]{2,1,0:T(8,128)} %param.16) | non-fusion elementwise | flops 262144 | bytes 1572864 | tf_op jit(solution)/shard_map/convert_element_type | solution.py:52
  6.0 1.0 %reshape.190 = bf16[2048,128]{1,0:T(8,128)(2,1)} reshape(bf16[4,256,256]{2,1,0:T(8,128)(2,1)S(1)} %convert_element_type.31) | data formatting | bytes 1048576 | tf_op jit(solution)/shard_map/reshape | solution.py:52
  7.0 12.0 %while.24 = (s32[]{:T(128)}, f32[2,2,6,4,128]{4,3,1,0,2:T(4,128)S(1)}, s32[2,2,32,6,4]{2,4,3,1,0:T(4,128)S(1)}, s32[2,2]{1,0:T(2,128)S(1)}, bf16[2048,128]{1,0:T...) while((s32[]{:T(128)}, ...), condition=%wide.region_1.2_spmd.clone, body=%wide.region_0.1_spmd.clone.sunk | while | flops 997396544 | bytes 7703549 | solution.py:113
  7.0 0.1 iota_compare_fusion.8
  7.0 3.8 %fusion.102 = bf16[2,32,6,4,128]{4,1,3,2,0:T(8,128)(2,1)S(1)} fusion(s32[2,32,6,4]{1,3,2,0:T(4,128)S(1)} %dynamic-slice_bitcast_fusion.6, pred[2,32]{1,0:T(4,128)(4,1)S(1)} %iota_compare_fusion.8, bf16[2048,128]{1,0:T(8,128)(2,1)} %get-tuple-element.373), kind=kOutput, calls=%fused_computation.14.clone.1 | convolution fusion | flops 811794432 | bytes 923712 | tf_op jit(solution)/shard_map/while/body/eval_jaxpr/akwqn,nv->akwqv/dot_general | solution.py:102
  10.8 0.8 convert_bitcast_fusion.4
  11.6 1.3 %fusion.103 = f32[1,2,6,4,128]{4,2,3,1,0:T(8,128)S(1)} fusion(bf16[2,32,128,128,1]{3,1,2,0,4:T(8,128)(2,1)S(1)} %convert_bitcast_fusion.4, bf16[2,32,6,4,128]{4,1,3,2,0:T(8,128)(2,1)S(1)} %fusion.102), kind=kOutput, calls=%fused_computation.15.clone.1 | convolution fusion | flops 50331648 | bytes 2514944 | tf_op jit(solution)/shard_map/while/body/eval_jaxpr/akdv,akwqv->awqd/dot_general | solution.py:106
  13.0 0.1 iota_compare_fusion.8
  13.1 3.8 %fusion.102 = bf16[2,32,6,4,128]{4,1,3,2,0:T(8,128)(2,1)S(1)} fusion(s32[2,32,6,4]{1,3,2,0:T(4,128)S(1)} %dynamic-slice_bitcast_fusion.6, pred[2,32]{1,0:T(4,128)(4,1)S(1)} %iota_compare_fusion.8, bf16[2048,128]{1,0:T(8,128)(2,1)} %get-tuple-element.373), kind=kOutput, calls=%fused_computation.14.clone.1 | convolution fusion | flops 811794432 | bytes 923712 | tf_op jit(solution)/shard_map/while/body/eval_jaxpr/akwqn,nv->akwqv/dot_general | solution.py:102
  16.9 0.8 convert_bitcast_fusion.4
  17.6 1.3 %fusion.103 = f32[1,2,6,4,128]{4,2,3,1,0:T(8,128)S(1)} fusion(bf16[2,32,128,128,1]{3,1,2,0,4:T(8,128)(2,1)S(1)} %convert_bitcast_fusion.4, bf16[2,32,6,4,128]{4,1,3,2,0:T(8,128)(2,1)S(1)} %fusion.102), kind=kOutput, calls=%fused_computation.15.clone.1 | convolution fusion | flops 50331648 | bytes 2514944 | tf_op jit(solution)/shard_map/while/body/eval_jaxpr/akdv,akwqv->awqd/dot_general | solution.py:106
  19.0 13.2 %psum.7 = f32[4,6,512]{2,0,1:T(4,128)S(1)} all-reduce(f32[4,6,512]{2,0,1:T(4,128)S(1)} %reshape_reshape.3), channel_id=1, replica_groups=mesh['grp'=2,'gz'=4,'gx'=2,'row'=2] {'gx','row'}, use_global_device_ids=true, to_apply=%region_2.3 | all-reduce | flops 12288 | bytes 98304 | tf_op jit(solution)/shard_map/psum | solution.py:119
  32.2 3.5 %collective-permute-start = (f32[4,2,512]{2,0,1:T(4,128)S(1)}, f32[4,2,512]{2,0,1:T(4,128)S(1)}, u32[]{:S(2)}, u32[]{:S(2)}) collective-permute-start(f32[4,2,512]{2,0,1:T(4,128)S(1)} %slice.82), channel_id=1, source_target_pairs={{0,4},{4,8},{8,12},{1,5},{5,9},{9,13},{2,6},{6,10},{10,14},{3,7},{... | collective-permute-start | bytes 49160 | tf_op jit(solution)/shard_map/ppermute | solution.py:16
  35.8 0.1 copy.81
  36.0 0.8 reshape.209
  36.7 3.9 %all-to-all-start = ((f32[1,4,768]{2,0,1:T(1,128)}), f32[1,4,768]{2,0,1:T(1,128)S(1)}, u32[]{:S(2)}, u32[]{:S(2)}) async-start(f32[1,4,768]{2,0,1:T(1,128)} %reshape.209), calls=%async_computation | async-start | bytes 24576 | tf_op jit(solution)/shard_map/all_to_all | solution.py:82
  40.7 0.3 copy.92
  40.9 0.2 copy.86
  41.1 0.8 reshape.210
  41.9 1.3 %collective-permute-start.1 = (f32[4,2,512]{2,0,1:T(4,128)S(1)}, f32[4,2,512]{2,0,1:T(4,128)S(1)}, u32[]{:S(2)}, u32[]{:S(2)}) collective-permute-start(f32[4,2,512]{2,0,1:T(4,128)S(1)} %get-tuple-element.261), channel_id=1, source_target_pairs={{4,0},{8,4},{12,8},{5,1},{9,5},{13,9},{6,2},{10,6},{14,10},{7,3},{... | collective-permute-start | bytes 49160 | tf_op jit(solution)/shard_map/ppermute | solution.py:18
  43.2 3.0 %all-to-all-done = f32[1,4,768]{2,0,1:T(1,128)S(1)} async-done(((f32[1,4,768]{2,0,1:T(1,128)}), f32[1,4,768]{2,0,1:T(1,128)S(1)}, u32[]{:S(2)}, u32[]{:S(2)}) %all-to-all-start) | async-done | bytes 12320 | tf_op jit(solution)/shard_map/all_to_all | solution.py:82
  46.2 3.3 %all-to-all-start.1 = ((f32[1,4,768]{2,0,1:T(1,128)}), f32[1,4,768]{2,0,1:T(1,128)S(1)}, u32[]{:S(2)}, u32[]{:S(2)}) async-start(f32[1,4,768]{2,0,1:T(1,128)} %reshape.210), calls=%async_computation.1 | async-start | bytes 24576 | tf_op jit(solution)/shard_map/all_to_all | solution.py:81
  49.5 5.2 %all-gather = f32[1,4,3072]{2,0,1:T(1,128)S(1)} all-gather(f32[1,4,768]{2,0,1:T(1,128)S(1)} %all-to-all-done), channel_id=2, replica_groups=mesh['grp'=2,'gz'=4,'gx'=2,'row'=2] {'gx','row'}, dimensions={2}, use_global_device_ids=true | all-gather | bytes 61440 | tf_op jit(solution)/shard_map/all_gather | solution.py:88
  54.7 0.1 reduce.5
  54.8 1.0 %reshape.184 = f32[4,512,6]{2,1,0:T(8,128)S(1)} reshape(f32[4,3072]{1,0:T(4,128)S(1)} %reduce.5) | data formatting | bytes 98304 | tf_op jit(solution)/shard_map/reshape | solution.py:93
  55.9 0.3 copy.83
  56.2 5.4 %all-gather.1 = f32[1,4,3072]{2,0,1:T(1,128)S(1)} all-gather(f32[1,4,768]{2,0,1:T(1,128)S(1)} %all-to-all-done.1), channel_id=3, replica_groups=mesh['grp'=2,'gz'=4,'gx'=2,'row'=2] {'gx','row'}, dimensions={2}, use_global_device_ids=true | all-gather | bytes 61440 | tf_op jit(solution)/shard_map/all_gather | solution.py:85
  61.6 0.1 reduce.6
  61.7 1.0 %reshape.189 = f32[4,512,6]{2,1,0:T(8,128)S(1)} reshape(f32[4,3072]{1,0:T(4,128)S(1)} %reduce.6) | data formatting | bytes 98304 | tf_op jit(solution)/shard_map/reshape | solution.py:92
  62.8 0.3 copy.88
  63.2 24.8 %while.25 = (s32[]{:T(128)}, f32[2048,128]{1,0:T(8,128)}, s32[2,2,32,6,4]{2,3,4,1,0:T(8,128)S(1)}, s32[2,2]{1,0:T(2,128)S(1)}, bf16[2,2,6,4,128]{4,3,1,0,2:T(4,1...) while((s32[]{:T(128)}, f32[2048,128]{1,0:T(8,128)}, ...), condition=%wide.region_4.5_spmd.clone, body=%wide.region_3.4_spmd.clone.sunk | while | flops 1810370560 | bytes 12907599 | solution.py:149
  63.2 0.7 convert_bitcast_fusion.5
  64.0 0.7 fusion.113
  64.8 4.7 %fusion.114 = f32[2048,128]{1,0:T(8,128)} fusion(s32[2,32,6,4]{1,2,3,0:T(8,128)S(1)} %dynamic-slice_bitcast_fusion.7, pred[2,32]{1,0:T(4,128)(4,1)S(1)} %iota_compare_fusion.9, f32[2,6,4,32,128]{4,1,3,2,0:T(8,128)S(1)} %fusion.113), kind=kOutput, calls=%fused_computation.36.clone.1 | convolution fusion | flops 811597824 | bytes 1841216 | tf_op jit(solution)/shard_map/while/body/eval_jaxpr/akwqn,akwqv->nv/dot_general | solution.py:138
  69.5 5.9 %fusion.115 = f32[2048,128]{1,0:T(8,128)} fusion(f32[2048,128]{1,0:T(8,128)} %fusion.114, s32[2,32,6,4]{1,2,3,0:T(8,128)S(1)} %dynamic-slice_bitcast_fusion.7, pred[2,32]{1,0:T(4,128)(4,1)S(1)} %iota_compare_fusion.9, f32[2048,128]{1,0:T(8,128)} %get-tuple-element.387, pred[]{:T(512)S(6)} %compare.16, f32[2,6,4,32,128]{4,1,3,2,0:T(8,128)S(1)} %fusion.113), kind=kOutput, calls=%fused_computation.39.clone.1 | convolution fusion | flops 813170688 | bytes 3938369 | tf_op jit(solution)/shard_map/while/body/eval_jaxpr/akwqn,akwqv->nv/dot_general | solution.py:141
  75.5 0.8 convert_bitcast_fusion.5
  76.2 0.7 fusion.113
  77.1 4.7 %fusion.114 = f32[2048,128]{1,0:T(8,128)} fusion(s32[2,32,6,4]{1,2,3,0:T(8,128)S(1)} %dynamic-slice_bitcast_fusion.7, pred[2,32]{1,0:T(4,128)(4,1)S(1)} %iota_compare_fusion.9, f32[2,6,4,32,128]{4,1,3,2,0:T(8,128)S(1)} %fusion.113), kind=kOutput, calls=%fused_computation.36.clone.1 | convolution fusion | flops 811597824 | bytes 1841216 | tf_op jit(solution)/shard_map/while/body/eval_jaxpr/akwqn,akwqv->nv/dot_general | solution.py:138
  81.8 6.2 %fusion.115 = f32[2048,128]{1,0:T(8,128)} fusion(f32[2048,128]{1,0:T(8,128)} %fusion.114, s32[2,32,6,4]{1,2,3,0:T(8,128)S(1)} %dynamic-slice_bitcast_fusion.7, pred[2,32]{1,0:T(4,128)(4,1)S(1)} %iota_compare_fusion.9, f32[2048,128]{1,0:T(8,128)} %get-tuple-element.387, pred[]{:T(512)S(6)} %compare.16, f32[2,6,4,32,128]{4,1,3,2,0:T(8,128)S(1)} %fusion.113), kind=kOutput, calls=%fused_computation.39.clone.1 | convolution fusion | flops 813170688 | bytes 3938369 | tf_op jit(solution)/shard_map/while/body/eval_jaxpr/akwqn,akwqv->nv/dot_general | solution.py:141
  88.0 1.7 %reshape.193 = f32[4,256,256]{2,1,0:T(8,128)S(1)} reshape(f32[2048,128]{1,0:T(8,128)} %get-tuple-element.124) | data formatting | bytes 2097152 | tf_op jit(solution)/shard_map/reshape | solution.py:152
  89.7 0.2 copy-done.1
  89.9 1.2 %multiply_add_fusion = f32[4,256,256]{2,1,0:T(8,128)} fusion(f32[4,256,256]{2,1,0:T(8,128)S(1)} %copy-done, f32[4,256,256]{2,1,0:T(8,128)S(1)} %copy-done.1, f32[4,256,256]{2,1,0:T(8,128)S(1)} %reshape.193), kind=kLoop, calls=%fused_computation.60 | loop fusion | flops 524288 | bytes 4194304 | tf_op jit(solution)/shard_map/add | solution.py:152
  (52 shorter events, 0.5 us)
Async XLA Ops:
  0.0 3.0 %copy-start.3 = (s32[1,1,1,4,768]{4,3,2,1,0:T(4,128)S(1)}, s32[1,1,1,4,768]{4,3,2,1,0:T(4,128)}, u32[]{:S(2)}) copy-start(s32[1,1,1,4,768]{4,3,2,1,0:T(4,128)} %param.19) | copy-start | bytes 36868
  0.0 3.9 %copy-start.6 = (s32[1,1,1,4]{3,2,1,0:T(1,128)S(1)}, s32[1,1,1,4]{3,2,1,0:T(1,128)}, u32[]{:S(2)}) copy-start(s32[1,1,1,4]{3,2,1,0:T(1,128)} %param.20) | copy-start | bytes 52
  3.0 4.0 %copy-start.2 = (s32[1,1,1,4,32]{4,3,2,1,0:T(4,128)S(1)}, s32[1,1,1,4,32]{4,3,2,1,0:T(4,128)}, u32[]{:S(2)}) copy-start(s32[1,1,1,4,32]{4,3,2,1,0:T(4,128)} %param.18) | copy-start | bytes 1540
  6.9 28.8 %copy-start.4 = (f32[1,128,16]{1,2,0:T(8,128)S(1)}, f32[1,128,16]{1,2,0:T(8,128)}, u32[]{:S(2)}) copy-start(f32[1,128,16]{1,2,0:T(8,128)} %param.22) | copy-start | bytes 24580
  6.9 33.7 %copy-start.5 = (f32[1,128,16]{1,2,0:T(8,128)S(1)}, f32[1,128,16]{1,2,0:T(8,128)}, u32[]{:S(2)}) copy-start(f32[1,128,16]{1,2,0:T(8,128)} %param.21) | copy-start | bytes 24580
  32.2 9.7 %collective-permute-start = (f32[4,2,512]{2,0,1:T(4,128)S(1)}, f32[4,2,512]{2,0,1:T(4,128)S(1)}, u32[]{:S(2)}, u32[]{:S(2)}) collective-permute-start(f32[4,2,512]{2,0,1:T(4,128)S(1)} %slice.82), channel_id=1, source_target_pairs={{0,4},{4,8},{8,12},{1,5},{5,9},{9,13},{2,6},{6,10},{10,14},{3,7},{... | collective-permute-start | bytes 49160 | tf_op jit(solution)/shard_map/ppermute | solution.py:16
  36.7 9.5 %all-to-all-start = ((f32[1,4,768]{2,0,1:T(1,128)}), f32[1,4,768]{2,0,1:T(1,128)S(1)}, u32[]{:S(2)}, u32[]{:S(2)}) async-start(f32[1,4,768]{2,0,1:T(1,128)} %reshape.209), calls=%async_computation | async-start | bytes 24576 | tf_op jit(solution)/shard_map/all_to_all | solution.py:82
  41.9 21.2 %collective-permute-start.1 = (f32[4,2,512]{2,0,1:T(4,128)S(1)}, f32[4,2,512]{2,0,1:T(4,128)S(1)}, u32[]{:S(2)}, u32[]{:S(2)}) collective-permute-start(f32[4,2,512]{2,0,1:T(4,128)S(1)} %get-tuple-element.261), channel_id=1, source_target_pairs={{4,0},{8,4},{12,8},{5,1},{9,5},{13,9},{6,2},{10,6},{14,10},{7,3},{... | collective-permute-start | bytes 49160 | tf_op jit(solution)/shard_map/ppermute | solution.py:18
  46.2 10.0 %all-to-all-start.1 = ((f32[1,4,768]{2,0,1:T(1,128)}), f32[1,4,768]{2,0,1:T(1,128)S(1)}, u32[]{:S(2)}, u32[]{:S(2)}) async-start(f32[1,4,768]{2,0,1:T(1,128)} %reshape.210), calls=%async_computation.1 | async-start | bytes 24576 | tf_op jit(solution)/shard_map/all_to_all | solution.py:81
  88.0 1.7 %copy-start = (f32[4,256,256]{2,1,0:T(8,128)S(1)}, f32[4,256,256]{2,1,0:T(8,128)}, u32[]{:S(2)}) copy-start(f32[4,256,256]{2,1,0:T(8,128)} %param.16) | copy-start | bytes 3145732
  88.0 1.9 %copy-start.1 = (f32[4,256,256]{2,1,0:T(8,128)S(1)}, f32[4,256,256]{2,1,0:T(8,128)}, u32[]{:S(2)}) copy-start(f32[4,256,256]{2,1,0:T(8,128)} %param.23) | copy-start | bytes 3145732
where the time goes:
time: 91.6 us; the launch traced here: 91.1 us
  matrix products  36.2 us (40%)
  blocking collectives  23.8 us (26%)
  local copies, waits for them, and re-layouts  12 us (13%)
  starting transfers between devices  11.9 us (13%)
  other arithmetic  3.73 us (4%)
  waiting for transfers between devices  3.01 us (3%)
    psum x1, blocking collectives, on_device(): total_proj = lax.psum(partial_value, ('gx', 'row'))  13.2 us
    dot_general x2, matrix products, slot_step(): jnp.einsum('akwqn,akwqv->nv', block_hot, lower_part, preferred_element_ty...  12.2 us
    dot_general x2, matrix products, slot_step(): jnp.einsum('akwqn,akwqv->nv', block_hot, upper_part, preferred_element_ty...  9.4 us
    dot_general x2, matrix products, slot_step(): jnp.einsum('akwqn,nv->akwqv', block_hot, voxel_rows, preferred_element_ty...  7.55 us
    all_gather x1, blocking collectives, on_device(): lax.all_gather(arrived[0].reshape(angle_count, local_cols * window), ('gx...  5.38 us
    all_gather x1, blocking collectives, on_device(): lax.all_gather(arrived[1].reshape(angle_count, local_cols * window), ('gx...  5.19 us
    unnamed x18, local copies, waits for them, and re-layouts  4.17 us
    all_to_all x1, starting transfers between devices, on_device(): lax.all_to_all(norm_win, 'gz', split_axis=1, concat_axis=0, tiled=True)  3.86 us
  transfers between devices with their start and end apart: 4, of which 1 were waited for; matrix products, arithmetic and copies ran while one was open for 6% of the time, Pallas kernels for 0%

commit v1 on v0

--- a/solution.py
+++ b/solution.py
@@ -116,7 +116,7 @@
     partial_value = stacked.reshape((angle_count,) + out_shape).reshape(
         angle_count, window, det_width
     )
-    total_proj = lax.psum(partial_value, ("gx", "row"))
+    total_proj = jnp.sum(lax.all_gather(partial_value, ("gx", "row")), axis=0)
     extended = extended_2(total_proj, (("gz", 1),), 2)
     folded = (
         total_proj.at[:, :2].add(extended[:, :2]).at[:, window - 2 :].add(extended[:, window + 2 :])

time: 91.6 us -> 85.4 us (0.932)
  blocking collectives: 23.8 us -> 17.4 us
    psum x1 -> x0, blocking collectives: 13.2 us -> none  [on_device(): total_proj = lax.psum(partial_value, ('gx', 'row'))]
    all_gather x0 -> x1, blocking collectives: none -> 6.86 us  [on_device(): total_proj = jnp.sum(lax.all_gather(partial_value, ('gx', 'row')), axis=0)]
where the time goes in v1:
time: 85.4 us; the launch traced here: 84.9 us
  matrix products  36.2 us (42%)
  blocking collectives  17.4 us (20%)
  starting transfers between devices  12.1 us (14%)
  local copies, waits for them, and re-layouts  12 us (14%)
  other arithmetic  3.77 us (4%)
  waiting for transfers between devices  3.01 us (4%)
    dot_general x2, matrix products, slot_step(): jnp.einsum('akwqn,akwqv->nv', block_hot, lower_part, preferred_element_ty...  12.2 us
    dot_general x2, matrix products, slot_step(): jnp.einsum('akwqn,akwqv->nv', block_hot, upper_part, preferred_element_ty...  9.4 us
    dot_general x2, matrix products, slot_step(): jnp.einsum('akwqn,nv->akwqv', block_hot, voxel_rows, preferred_element_ty...  7.55 us
    all_gather x1, blocking collectives, on_device(): total_proj = jnp.sum(lax.all_gather(partial_value, ('gx', 'row')), axis=0)  6.86 us
    all_gather x1, blocking collectives, on_device(): lax.all_gather(arrived[0].reshape(angle_count, local_cols * window), ('gx...  5.38 us
    all_gather x1, blocking collectives, on_device(): lax.all_gather(arrived[1].reshape(angle_count, local_cols * window), ('gx...  5.19 us
    unnamed x18, local copies, waits for them, and re-layouts  4.17 us
    all_to_all x1, starting transfers between devices, on_device(): lax.all_to_all(norm_win, 'gz', split_axis=1, concat_axis=0, tiled=True)  3.85 us
  transfers between devices with their start and end apart: 4, of which 1 were waited for; matrix products, arithmetic and copies ran while one was open for 6% of the time, Pallas kernels for 0%

profile of v1, /device:TPU:0, one launch (start us, length us, event | category | flops | bytes accessed | tf_op | source)
XLA Modules:
  0.0 84.9 jit_solution(381643714209089378)
XLA Ops:
  0.0 3.0 %copy.107 = bf16[64,128,128]{2,0,1:T(8,128)(2,1)S(1)} copy(bf16[64,128,128]{2,1,0:T(8,128)(2,1)} %param.17) | data formatting | bytes 4194304
  3.0 0.2 reshape.178
  3.2 0.2 copy.106
  3.4 0.5 broadcast.83
  3.9 0.7 reduce.9
  4.6 0.1 reshape.179
  4.7 1.3 %convert_element_type.31 = bf16[4,256,256]{2,1,0:T(8,128)(2,1)S(1)} convert(f32[4,256,256]{2,1,0:T(8,128)} %param.16) | non-fusion elementwise | flops 262144 | bytes 1572864 | tf_op jit(solution)/shard_map/convert_element_type | solution.py:52
  6.0 1.0 %reshape.190 = bf16[2048,128]{1,0:T(8,128)(2,1)} reshape(bf16[4,256,256]{2,1,0:T(8,128)(2,1)S(1)} %convert_element_type.31) | data formatting | bytes 1048576 | tf_op jit(solution)/shard_map/reshape | solution.py:52
  7.0 12.0 %while.24 = (s32[]{:T(128)}, f32[2,2,6,4,128]{4,3,1,0,2:T(4,128)S(1)}, s32[2,2,32,6,4]{2,4,3,1,0:T(4,128)S(1)}, s32[2,2]{1,0:T(2,128)S(1)}, bf16[2048,128]{1,0:T...) while((s32[]{:T(128)}, ...), condition=%wide.region_1.2_spmd.clone, body=%wide.region_0.1_spmd.clone.sunk | while | flops 997396544 | bytes 7703549 | solution.py:113
  7.0 0.1 iota_compare_fusion.8
  7.0 3.8 %fusion.102 = bf16[2,32,6,4,128]{4,1,3,2,0:T(8,128)(2,1)S(1)} fusion(s32[2,32,6,4]{1,3,2,0:T(4,128)S(1)} %dynamic-slice_bitcast_fusion.6, pred[2,32]{1,0:T(4,128)(4,1)S(1)} %iota_compare_fusion.8, bf16[2048,128]{1,0:T(8,128)(2,1)} %get-tuple-element.387), kind=kOutput, calls=%fused_computation.14.clone.1 | convolution fusion | flops 811794432 | bytes 923712 | tf_op jit(solution)/shard_map/while/body/eval_jaxpr/akwqn,nv->akwqv/dot_general | solution.py:102
  10.8 0.8 convert_bitcast_fusion.4
  11.6 1.3 %fusion.103 = f32[1,2,6,4,128]{4,2,3,1,0:T(8,128)S(1)} fusion(bf16[2,32,128,128,1]{3,1,2,0,4:T(8,128)(2,1)S(1)} %convert_bitcast_fusion.4, bf16[2,32,6,4,128]{4,1,3,2,0:T(8,128)(2,1)S(1)} %fusion.102), kind=kOutput, calls=%fused_computation.15.clone.1 | convolution fusion | flops 50331648 | bytes 2514944 | tf_op jit(solution)/shard_map/while/body/eval_jaxpr/akdv,akwqv->awqd/dot_general | solution.py:106
  13.0 0.1 iota_compare_fusion.8
  13.1 3.8 %fusion.102 = bf16[2,32,6,4,128]{4,1,3,2,0:T(8,128)(2,1)S(1)} fusion(s32[2,32,6,4]{1,3,2,0:T(4,128)S(1)} %dynamic-slice_bitcast_fusion.6, pred[2,32]{1,0:T(4,128)(4,1)S(1)} %iota_compare_fusion.8, bf16[2048,128]{1,0:T(8,128)(2,1)} %get-tuple-element.387), kind=kOutput, calls=%fused_computation.14.clone.1 | convolution fusion | flops 811794432 | bytes 923712 | tf_op jit(solution)/shard_map/while/body/eval_jaxpr/akwqn,nv->akwqv/dot_general | solution.py:102
  16.9 0.8 convert_bitcast_fusion.4
  17.6 1.3 %fusion.103 = f32[1,2,6,4,128]{4,2,3,1,0:T(8,128)S(1)} fusion(bf16[2,32,128,128,1]{3,1,2,0,4:T(8,128)(2,1)S(1)} %convert_bitcast_fusion.4, bf16[2,32,6,4,128]{4,1,3,2,0:T(8,128)(2,1)S(1)} %fusion.102), kind=kOutput, calls=%fused_computation.15.clone.1 | convolution fusion | flops 50331648 | bytes 2514944 | tf_op jit(solution)/shard_map/while/body/eval_jaxpr/akdv,akwqv->awqd/dot_general | solution.py:106
  19.0 6.9 %all_gather.11 = f32[4,4,6,512]{3,1,2,0:T(4,128)S(1)} all-gather(f32[1,4,6,512]{3,1,2,0:T(4,128)S(1)} %all_gather_reshape_reshape.3), channel_id=1, replica_groups=mesh['grp'=2,'gz'=4,'gx'=2,'row'=2] {'gx','row'}, dimensions={0}, use_global_device_ids=true | all-gather | bytes 245760 | tf_op jit(solution)/shard_map/all_gather | solution.py:119
  25.9 3.7 %collective-permute-start = (f32[4,2,512]{2,0,1:T(4,128)S(1)}, f32[4,2,512]{2,0,1:T(4,128)S(1)}, u32[]{:S(2)}, u32[]{:S(2)}) collective-permute-start(f32[4,2,512]{2,0,1:T(4,128)S(1)} %slice.82), channel_id=1, source_target_pairs={{0,4},{4,8},{8,12},{1,5},{5,9},{9,13},{2,6},{6,10},{10,14},{3,7},{... | collective-permute-start | bytes 49160 | tf_op jit(solution)/shard_map/ppermute | solution.py:16
  29.7 0.1 copy.98
  29.8 0.8 reshape.209
  30.6 3.9 %all-to-all-start = ((f32[1,4,768]{2,0,1:T(1,128)}), f32[1,4,768]{2,0,1:T(1,128)S(1)}, u32[]{:S(2)}, u32[]{:S(2)}) async-start(f32[1,4,768]{2,0,1:T(1,128)} %reshape.209), calls=%async_computation | async-start | bytes 24576 | tf_op jit(solution)/shard_map/all_to_all | solution.py:82
  34.5 0.3 copy.109
  34.8 0.2 copy.103
  35.0 0.8 reshape.210
  35.8 1.3 %collective-permute-start.1 = (f32[4,2,512]{2,0,1:T(4,128)S(1)}, f32[4,2,512]{2,0,1:T(4,128)S(1)}, u32[]{:S(2)}, u32[]{:S(2)}) collective-permute-start(f32[4,2,512]{2,0,1:T(4,128)S(1)} %get-tuple-element.275), channel_id=1, source_target_pairs={{4,0},{8,4},{12,8},{5,1},{9,5},{13,9},{6,2},{10,6},{14,10},{7,3},{... | collective-permute-start | bytes 49160 | tf_op jit(solution)/shard_map/ppermute | solution.py:18
  37.1 3.0 %all-to-all-done = f32[1,4,768]{2,0,1:T(1,128)S(1)} async-done(((f32[1,4,768]{2,0,1:T(1,128)}), f32[1,4,768]{2,0,1:T(1,128)S(1)}, u32[]{:S(2)}, u32[]{:S(2)}) %all-to-all-start) | async-done | bytes 12320 | tf_op jit(solution)/shard_map/all_to_all | solution.py:82
  40.1 3.3 %all-to-all-start.1 = ((f32[1,4,768]{2,0,1:T(1,128)}), f32[1,4,768]{2,0,1:T(1,128)S(1)}, u32[]{:S(2)}, u32[]{:S(2)}) async-start(f32[1,4,768]{2,0,1:T(1,128)} %reshape.210), calls=%async_computation.1 | async-start | bytes 24576 | tf_op jit(solution)/shard_map/all_to_all | solution.py:81
  43.4 5.2 %all-gather = f32[1,4,3072]{2,0,1:T(1,128)S(1)} all-gather(f32[1,4,768]{2,0,1:T(1,128)S(1)} %all-to-all-done), channel_id=2, replica_groups=mesh['grp'=2,'gz'=4,'gx'=2,'row'=2] {'gx','row'}, dimensions={2}, use_global_device_ids=true | all-gather | bytes 61440 | tf_op jit(solution)/shard_map/all_gather | solution.py:88
  48.6 0.1 reduce.5
  48.7 1.0 %reshape.184 = f32[4,512,6]{2,1,0:T(8,128)S(1)} reshape(f32[4,3072]{1,0:T(4,128)S(1)} %reduce.5) | data formatting | bytes 98304 | tf_op jit(solution)/shard_map/reshape | solution.py:93
  49.7 0.3 copy.100
  50.1 5.4 %all-gather.1 = f32[1,4,3072]{2,0,1:T(1,128)S(1)} all-gather(f32[1,4,768]{2,0,1:T(1,128)S(1)} %all-to-all-done.1), channel_id=3, replica_groups=mesh['grp'=2,'gz'=4,'gx'=2,'row'=2] {'gx','row'}, dimensions={2}, use_global_device_ids=true | all-gather | bytes 61440 | tf_op jit(solution)/shard_map/all_gather | solution.py:85
  55.5 0.1 reduce.6
  55.6 1.0 %reshape.189 = f32[4,512,6]{2,1,0:T(8,128)S(1)} reshape(f32[4,3072]{1,0:T(4,128)S(1)} %reduce.6) | data formatting | bytes 98304 | tf_op jit(solution)/shard_map/reshape | solution.py:92
  56.6 0.3 copy.105
  57.0 24.8 %while.25 = (s32[]{:T(128)}, f32[2048,128]{1,0:T(8,128)}, s32[2,2,32,6,4]{2,3,4,1,0:T(8,128)S(1)}, s32[2,2]{1,0:T(2,128)S(1)}, bf16[2,2,6,4,128]{4,3,1,0,2:T(4,1...) while((s32[]{:T(128)}, f32[2048,128]{1,0:T(8,128)}, ...), condition=%wide.region_4.5_spmd.clone, body=%wide.region_3.4_spmd.clone.sunk | while | flops 1810370560 | bytes 12907599 | solution.py:149
  57.1 0.8 convert_bitcast_fusion.5
  57.9 0.7 fusion.113
  58.7 4.7 %fusion.114 = f32[2048,128]{1,0:T(8,128)} fusion(s32[2,32,6,4]{1,2,3,0:T(8,128)S(1)} %dynamic-slice_bitcast_fusion.7, pred[2,32]{1,0:T(4,128)(4,1)S(1)} %iota_compare_fusion.9, f32[2,6,4,32,128]{4,1,3,2,0:T(8,128)S(1)} %fusion.113), kind=kOutput, calls=%fused_computation.36.clone.1 | convolution fusion | flops 811597824 | bytes 1841216 | tf_op jit(solution)/shard_map/while/body/eval_jaxpr/akwqn,akwqv->nv/dot_general | solution.py:138
  63.4 5.9 %fusion.115 = f32[2048,128]{1,0:T(8,128)} fusion(f32[2048,128]{1,0:T(8,128)} %fusion.114, s32[2,32,6,4]{1,2,3,0:T(8,128)S(1)} %dynamic-slice_bitcast_fusion.7, pred[2,32]{1,0:T(4,128)(4,1)S(1)} %iota_compare_fusion.9, f32[2048,128]{1,0:T(8,128)} %get-tuple-element.401, pred[]{:T(512)S(6)} %compare.16, f32[2,6,4,32,128]{4,1,3,2,0:T(8,128)S(1)} %fusion.113), kind=kOutput, calls=%fused_computation.39.clone.1 | convolution fusion | flops 813170688 | bytes 3938369 | tf_op jit(solution)/shard_map/while/body/eval_jaxpr/akwqn,akwqv->nv/dot_general | solution.py:141
  69.3 0.7 convert_bitcast_fusion.5
  70.1 0.7 fusion.113
  70.9 4.7 %fusion.114 = f32[2048,128]{1,0:T(8,128)} fusion(s32[2,32,6,4]{1,2,3,0:T(8,128)S(1)} %dynamic-slice_bitcast_fusion.7, pred[2,32]{1,0:T(4,128)(4,1)S(1)} %iota_compare_fusion.9, f32[2,6,4,32,128]{4,1,3,2,0:T(8,128)S(1)} %fusion.113), kind=kOutput, calls=%fused_computation.36.clone.1 | convolution fusion | flops 811597824 | bytes 1841216 | tf_op jit(solution)/shard_map/while/body/eval_jaxpr/akwqn,akwqv->nv/dot_general | solution.py:138
  75.6 6.2 %fusion.115 = f32[2048,128]{1,0:T(8,128)} fusion(f32[2048,128]{1,0:T(8,128)} %fusion.114, s32[2,32,6,4]{1,2,3,0:T(8,128)S(1)} %dynamic-slice_bitcast_fusion.7, pred[2,32]{1,0:T(4,128)(4,1)S(1)} %iota_compare_fusion.9, f32[2048,128]{1,0:T(8,128)} %get-tuple-element.401, pred[]{:T(512)S(6)} %compare.16, f32[2,6,4,32,128]{4,1,3,2,0:T(8,128)S(1)} %fusion.113), kind=kOutput, calls=%fused_computation.39.clone.1 | convolution fusion | flops 813170688 | bytes 3938369 | tf_op jit(solution)/shard_map/while/body/eval_jaxpr/akwqn,akwqv->nv/dot_general | solution.py:141
  81.9 1.7 %reshape.193 = f32[4,256,256]{2,1,0:T(8,128)S(1)} reshape(f32[2048,128]{1,0:T(8,128)} %get-tuple-element.124) | data formatting | bytes 2097152 | tf_op jit(solution)/shard_map/reshape | solution.py:152
  83.6 0.2 copy-done.1
  83.7 1.2 %multiply_add_fusion = f32[4,256,256]{2,1,0:T(8,128)} fusion(f32[4,256,256]{2,1,0:T(8,128)S(1)} %copy-done, f32[4,256,256]{2,1,0:T(8,128)S(1)} %copy-done.1, f32[4,256,256]{2,1,0:T(8,128)S(1)} %reshape.193), kind=kLoop, calls=%fused_computation.60 | loop fusion | flops 524288 | bytes 4194304 | tf_op jit(solution)/shard_map/add | solution.py:152
  (53 shorter events, 0.5 us)
Async XLA Ops:
  0.0 3.0 %copy-start.3 = (s32[1,1,1,4,768]{4,3,2,1,0:T(4,128)S(1)}, s32[1,1,1,4,768]{4,3,2,1,0:T(4,128)}, u32[]{:S(2)}) copy-start(s32[1,1,1,4,768]{4,3,2,1,0:T(4,128)} %param.19) | copy-start | bytes 36868
  0.0 3.9 %copy-start.6 = (s32[1,1,1,4]{3,2,1,0:T(1,128)S(1)}, s32[1,1,1,4]{3,2,1,0:T(1,128)}, u32[]{:S(2)}) copy-start(s32[1,1,1,4]{3,2,1,0:T(1,128)} %param.20) | copy-start | bytes 52
  3.0 4.0 %copy-start.2 = (s32[1,1,1,4,32]{4,3,2,1,0:T(4,128)S(1)}, s32[1,1,1,4,32]{4,3,2,1,0:T(4,128)}, u32[]{:S(2)}) copy-start(s32[1,1,1,4,32]{4,3,2,1,0:T(4,128)} %param.18) | copy-start | bytes 1540
  6.9 22.7 %copy-start.4 = (f32[1,128,16]{1,2,0:T(8,128)S(1)}, f32[1,128,16]{1,2,0:T(8,128)}, u32[]{:S(2)}) copy-start(f32[1,128,16]{1,2,0:T(8,128)} %param.22) | copy-start | bytes 24580
  6.9 27.5 %copy-start.5 = (f32[1,128,16]{1,2,0:T(8,128)S(1)}, f32[1,128,16]{1,2,0:T(8,128)}, u32[]{:S(2)}) copy-start(f32[1,128,16]{1,2,0:T(8,128)} %param.21) | copy-start | bytes 24580
  25.9 9.9 %collective-permute-start = (f32[4,2,512]{2,0,1:T(4,128)S(1)}, f32[4,2,512]{2,0,1:T(4,128)S(1)}, u32[]{:S(2)}, u32[]{:S(2)}) collective-permute-start(f32[4,2,512]{2,0,1:T(4,128)S(1)} %slice.82), channel_id=1, source_target_pairs={{0,4},{4,8},{8,12},{1,5},{5,9},{9,13},{2,6},{6,10},{10,14},{3,7},{... | collective-permute-start | bytes 49160 | tf_op jit(solution)/shard_map/ppermute | solution.py:16
  30.6 9.5 %all-to-all-start = ((f32[1,4,768]{2,0,1:T(1,128)}), f32[1,4,768]{2,0,1:T(1,128)S(1)}, u32[]{:S(2)}, u32[]{:S(2)}) async-start(f32[1,4,768]{2,0,1:T(1,128)} %reshape.209), calls=%async_computation | async-start | bytes 24576 | tf_op jit(solution)/shard_map/all_to_all | solution.py:82
  35.8 21.2 %collective-permute-start.1 = (f32[4,2,512]{2,0,1:T(4,128)S(1)}, f32[4,2,512]{2,0,1:T(4,128)S(1)}, u32[]{:S(2)}, u32[]{:S(2)}) collective-permute-start(f32[4,2,512]{2,0,1:T(4,128)S(1)} %get-tuple-element.275), channel_id=1, source_target_pairs={{4,0},{8,4},{12,8},{5,1},{9,5},{13,9},{6,2},{10,6},{14,10},{7,3},{... | collective-permute-start | bytes 49160 | tf_op jit(solution)/shard_map/ppermute | solution.py:18
  40.1 10.0 %all-to-all-start.1 = ((f32[1,4,768]{2,0,1:T(1,128)}), f32[1,4,768]{2,0,1:T(1,128)S(1)}, u32[]{:S(2)}, u32[]{:S(2)}) async-start(f32[1,4,768]{2,0,1:T(1,128)} %reshape.210), calls=%async_computation.1 | async-start | bytes 24576 | tf_op jit(solution)/shard_map/all_to_all | solution.py:81
  81.9 1.7 %copy-start = (f32[4,256,256]{2,1,0:T(8,128)S(1)}, f32[4,256,256]{2,1,0:T(8,128)}, u32[]{:S(2)}) copy-start(f32[4,256,256]{2,1,0:T(8,128)} %param.16) | copy-start | bytes 3145732
  81.9 1.9 %copy-start.1 = (f32[4,256,256]{2,1,0:T(8,128)S(1)}, f32[4,256,256]{2,1,0:T(8,128)}, u32[]{:S(2)}) copy-start(f32[4,256,256]{2,1,0:T(8,128)} %param.23) | copy-start | bytes 3145732
